TPU v7x, 32 devices: a whole 2x2x4 slice. The times are simulated.
32 devices in a mesh: cell: 16 (over z, y, x), gene: 2 (over core).
Axes of the slice: x: 2, y: 2, z: 4, core: 2. Of those that a mesh axis runs over, the one named last changes fastest.
Arguments:
- tiles: bfloat16 [2, 1024, 128, 128], P('gene', 'cell'), may hold values from -8 to 8
- tile_row: int32 [2, 1024], P('gene', 'cell'), may hold values from 0 to 7, as said below
- tile_col: int32 [2, 1024], P('gene', 'cell'), may hold values from 0 to 15
- tile_count: int32 [2, 16], P('gene', 'cell'), may hold values from 1 to 64, as said below
- start_basis: bfloat16 [64, 4096], P(None, 'gene'), may hold values from -0.09375 to 0.09375
Outputs:
- basis: bfloat16 [64, 16384], P(None, 'cell')
- loadings: float32 [64, 4096], P(None, ('gene', 'cell'))
Inputs may be any that keep to these rules, and one draw needn't show every extreme that they name: `tile_row`: tile row of each slot, within 0 to 7; the slots of one device name distinct (row, column) pairs. `tile_count`: slots in use; for each index of gene some device uses all 64.
All inputs are finite; a program needn't handle non-finite values.
Results may differ from a plain program's by a relative error of at most 0.018.
Values may be sent and summed in bfloat16 or wider, within the bound.
No kernel may reach another device: no remote copies, remote signals or barrier semaphores. Data moves between devices by JAX's collectives and lax.ppermute only.
A program may use at most 64 MiB of HBM per device.

v0:
```python
import jax
import jax.numpy as jnp
from jax import lax
from jax.sharding import PartitionSpec as P

ROW_BLOCKS = 8


def solve_lower(lower, right):
    return lax.linalg.triangular_solve(lower, right, left_side=True, lower=True)


def gram_of(scores):
    return jnp.dot(
        scores, scores.T, precision=lax.Precision.HIGHEST, preferred_element_type=jnp.float32
    )


def orthonormal(scores, first_total):
    first = first_total(gram_of(scores))
    lower_one = jnp.linalg.cholesky(first)
    return solve_lower(lower_one, scores)


def local(tiles, tile_row, tile_col, tile_count, start_basis):
    blocks_local = tiles[0]
    slot_count = blocks_local.shape[0]
    tile_size = blocks_local.shape[-1]
    width = start_basis.shape[0]
    gene_dev = start_basis.shape[1]
    gene_blocks = gene_dev // tile_size
    row_blocks = ROW_BLOCKS
    cell_dev = row_blocks * tile_size
    row_index = tile_row[0]
    col_index = tile_col[0]
    live = jnp.arange(slot_count) < tile_count[0, 0]
    row_target = jnp.where(live, row_index, row_blocks)
    col_target = jnp.where(live, col_index, gene_blocks)

    def first_total(gram):
        return lax.psum(gram, ("cell", "gene"))

    def merge_halves(partial_scores):
        return lax.psum_scatter(partial_scores, "gene", scatter_dimension=1, tiled=True)

    def scores_of(basis):
        picked = jnp.take(basis.reshape(width, gene_blocks, tile_size), col_index, axis=1)
        products = jnp.einsum(
            "ksg,srg->skr", picked, blocks_local, preferred_element_type=jnp.float32
        )
        summed = jax.ops.segment_sum(products, row_target, num_segments=row_blocks + 1)[:row_blocks]
        return merge_halves(jnp.transpose(summed, (1, 0, 2)).reshape(width, cell_dev))

    def loadings_of(ortho_half):
        picked = jnp.take(ortho_half.reshape(width, row_blocks, tile_size), row_index, axis=1)
        products = jnp.einsum(
            "ksr,srg->skg", picked, blocks_local, preferred_element_type=jnp.float32
        )
        summed = jax.ops.segment_sum(products, col_target, num_segments=gene_blocks + 1)[
            :gene_blocks
        ]
        return jnp.transpose(summed, (1, 0, 2)).reshape(width, gene_dev)

    ortho = orthonormal(scores_of(start_basis), first_total)
    ortho_half = ortho.astype(jnp.bfloat16)
    ortho_rows = lax.all_gather(ortho_half, "gene", axis=1, tiled=True)
    partial_value = loadings_of(ortho_rows)
    next_basis = lax.psum(partial_value, "cell").astype(jnp.bfloat16)
    ortho_two = orthonormal(scores_of(next_basis), first_total)
    scale = jnp.sqrt(jnp.float32(lax.axis_size("cell") * cell_dev))
    ortho_two_half = ortho_two.astype(jnp.bfloat16)
    basis_piece = (ortho_two * scale).astype(jnp.bfloat16)
    final_rows, basis = (
        lax.all_gather(ortho_two_half, "gene", axis=1, tiled=True),
        lax.all_gather(basis_piece, "gene", axis=1, tiled=True),
    )
    loadings = lax.psum_scatter(loadings_of(final_rows), "cell", scatter_dimension=1, tiled=True)
    return (basis, loadings)


def solution(mesh):
    return jax.shard_map(
        local,
        mesh=mesh,
        in_specs=(
            P("gene", "cell", None, None),
            P("gene", "cell"),
            P("gene", "cell"),
            P("gene", "cell"),
            P(None, "gene"),
        ),
        out_specs=(P(None, "cell"), P(None, ("gene", "cell"))),
        check_vma=False,
    )
```

profile of v0, /device:TPU:0, one launch (start us, length us, event | category | flops | bytes accessed | tf_op | source)
XLA Modules:
  0.0 349.9 jit_solution(15291023441210544630)
XLA Ops:
  7.2 0.0 reduce-scatter.4.cloned.1.call-start
  7.2 0.8 compare_select_fusion
  8.0 0.7 compare_and_fusion
  8.7 1.0 copy_bitcast_fusion.5
  10.4 0.7 gather_fusion
  11.2 2.9 fusion.6
  14.1 7.1 %scatter_fusion = f32[9,64,128]{2,1,0:T(8,128)S(1)} fusion(f32[9,64,128]{2,1,0:T(8,128)S(1)} %broadcast.69.clone, s32[64]{0:T(128)S(1)} %get-tuple-element.8, f32[64,64,128]{2,1,0:T(8,128)} %fusion.6), kind=kCustom, calls=%fused_computation.4 | custom fusion | flops 524288 | bytes 6291712 | tf_op jit(solution)/shard_map/scatter-add | solution.py:51
  21.2 0.7 copy_bitcast_fusion.3
  21.9 0.0 reduce-scatter.4.cloned.1.call-update
  21.9 0.0 reduce-scatter.6.cloned.1.call-start
  22.0 10.5 %reduce-scatter.4.cloned.1.call-done = f32[64,512]{1,0:T(8,128)} async-done(((f32[64,1024]{1,0:T(8,128)}), f32[64,512]{1,0:T(8,128)}) %reduce-scatter.4.cloned.1.call-update) | async-done | bytes 131088 | tf_op jit(solution)/shard_map/reduce_scatter | solution.py:44
  32.5 1.2 fusion.40
  33.8 40.5 %psum.21 = f32[64,64]{0,1:T(8,128)S(1)} all-reduce(f32[64,64]{0,1:T(8,128)S(1)} %fusion.40), channel_id=1, replica_groups=mesh['cell'=16,'gene'=2] {'cell','gene'}, use_global_device_ids=true, to_apply=%region_2.4 | all-reduce | flops 4096 | bytes 32768 | tf_op jit(solution)/shard_map/psum | solution.py:41
  74.3 0.1 copy.20
  74.4 5.8 %cholesky.44 = f32[64,64]{1,0:T(8,128)S(1)} custom-call(f32[64,64]{1,0:T(8,128)S(1)} %fusion.30), custom_call_target="Cholesky" | custom-call | tf_op jit(solution)/shard_map/jit(cholesky)/cholesky | solution.py:21
  80.3 0.6 compare_reduce_fusion.1
  80.9 0.7 fusion.24
  81.6 4.9 %custom-call.6 = f32[1,64,64]{1,2,0:T(8,128)S(1)} custom-call(f32[1,64,64]{2,1,0:T(8,128)S(1)} %fusion.24), custom_call_target="InvertDiagBlocksLowerTriangular" | custom-call | tf_op jit(solution)/shard_map/triangular_solve/custom-call.0 | solution.py:10
  86.5 1.2 convolution_convert_fusion
  87.7 1.9 all_gather.9
  89.7 0.7 gather_fusion.1
  90.4 2.1 fusion.4
  92.6 7.1 %scatter_fusion.1 = f32[17,64,128]{2,1,0:T(8,128)S(1)} fusion(f32[17,64,128]{2,1,0:T(8,128)S(1)} %broadcast.70.clone, s32[64]{0:T(128)S(1)} %get-tuple-element.9, f32[64,64,128]{2,1,0:T(8,128)} %fusion.4), kind=kCustom, calls=%fused_computation.5 | custom fusion | flops 524288 | bytes 6291712 | tf_op jit(solution)/shard_map/scatter-add | solution.py:59
  99.7 81.7 %all-reduce.1 = bf16[64,2048]{1,0:T(8,128)(2,1)S(1)} all-reduce(f32[64,2048]{1,0:T(8,128)S(1)} %copy_bitcast_fusion.1), channel_id=1, replica_groups=mesh['cell'=16,'gene'=2] {'cell'}, use_global_device_ids=true, to_apply=%region_6.11 | all-reduce | flops 131072 | bytes 786432 | tf_op jit(solution)/shard_map/psum | solution.py:68
  181.3 0.1 copy_bitcast_fusion.4
  181.4 0.8 gather_fusion.2
  182.2 2.9 fusion.2
  185.1 7.1 %scatter_fusion.2 = f32[9,64,128]{2,1,0:T(8,128)S(1)} fusion(f32[9,64,128]{2,1,0:T(8,128)S(1)} %broadcast.69, s32[64]{0:T(128)S(1)} %get-tuple-element.8, f32[64,64,128]{2,1,0:T(8,128)} %fusion.2), kind=kCustom, calls=%fused_computation.6 | custom fusion | flops 524288 | bytes 6291712 | tf_op jit(solution)/shard_map/scatter-add | solution.py:51
  192.2 0.7 copy_bitcast_fusion.2
  192.9 0.0 reduce-scatter.8.cloned.1.call-start
  192.9 4.2 %reduce-scatter.6.cloned.1.call-done = f32[64,512]{1,0:T(8,128)} async-done(((f32[64,1024]{1,0:T(8,128)}), f32[64,512]{1,0:T(8,128)}) %reduce-scatter.6.cloned.1.call-update) | async-done | bytes 131088 | tf_op jit(solution)/shard_map/reduce_scatter | solution.py:44
  197.1 1.2 fusion.41
  198.4 40.8 %psum.23 = f32[64,64]{0,1:T(8,128)S(1)} all-reduce(f32[64,64]{0,1:T(8,128)S(1)} %fusion.41), channel_id=1, replica_groups=mesh['cell'=16,'gene'=2] {'cell','gene'}, use_global_device_ids=true, to_apply=%region_9.14 | all-reduce | flops 4096 | bytes 32768 | tf_op jit(solution)/shard_map/psum | solution.py:41
  239.1 0.1 copy.26
  239.2 5.8 %cholesky.55 = f32[64,64]{1,0:T(8,128)S(1)} custom-call(f32[64,64]{1,0:T(8,128)S(1)} %fusion.28), custom_call_target="Cholesky" | custom-call | tf_op jit(solution)/shard_map/jit(cholesky)/cholesky | solution.py:21
  245.1 0.6 compare_reduce_fusion
  245.8 0.7 fusion.25
  246.4 4.9 %custom-call.7 = f32[1,64,64]{1,2,0:T(8,128)S(1)} custom-call(f32[1,64,64]{2,1,0:T(8,128)S(1)} %fusion.25), custom_call_target="InvertDiagBlocksLowerTriangular" | custom-call | tf_op jit(solution)/shard_map/triangular_solve/custom-call.0 | solution.py:10
  251.3 1.2 fusion.39
  252.6 1.9 all_gather.11
  254.5 0.7 gather_fusion.3
  255.2 2.1 fusion
  257.4 7.1 %scatter_fusion.3 = f32[17,64,128]{2,1,0:T(8,128)S(1)} fusion(f32[17,64,128]{2,1,0:T(8,128)S(1)} %broadcast.70, s32[64]{0:T(128)S(1)} %get-tuple-element.9, f32[64,64,128]{2,1,0:T(8,128)} %fusion), kind=kCustom, calls=%fused_computation.7 | custom fusion | flops 524288 | bytes 6291712 | tf_op jit(solution)/shard_map/scatter-add | solution.py:59
  264.4 0.8 copy_bitcast_fusion
  265.3 0.0 reduce-scatter.8.cloned.1.call-update
  265.3 1.9 all_gather.10
  267.2 75.5 %reduce-scatter.8.cloned.1.call-done = f32[64,128]{1,0:T(8,128)} async-done(((f32[64,2048]{1,0:T(8,128)}), f32[64,128]{1,0:T(8,128)}) %reduce-scatter.8.cloned.1.call-update) | async-done | bytes 32784 | tf_op jit(solution)/shard_map/reduce_scatter | solution.py:77
  342.7 0.7 copy.55
  (23 shorter events, 0.4 us)
Async XLA Ops:
  7.2 4.0 %copy-start = (bf16[1,64,128,128]{3,2,1,0:T(8,128)(2,1)S(1)}, bf16[1,64,128,128]{3,2,1,0:T(8,128)(2,1)}, u32[]{:S(2)}) copy-start(bf16[1,64,128,128]{3,2,1,0:T(8,128)(2,1)} %param.12) | copy-start | bytes 6291460
  7.2 4.0 %copy-start.1 = (s32[1,64]{1,0:T(1,128)S(1)}, s32[1,64]{1,0:T(1,128)}, u32[]{:S(2)}) copy-start(s32[1,64]{1,0:T(1,128)} %param.14) | copy-start | bytes 772
  7.2 4.0 %copy-start.2 = (s32[1,64]{1,0:T(1,128)S(1)}, s32[1,64]{1,0:T(1,128)}, u32[]{:S(2)}) copy-start(s32[1,64]{1,0:T(1,128)} %param.13) | copy-start | bytes 772
  7.2 25.3 %reduce-scatter.4.cloned.1.call-start = ((), (), s32[]{:S(2)}) async-start(), calls=%async_computation.3 | async-start | bytes 393216 | tf_op jit(solution)/shard_map/reduce_scatter | solution.py:44
  21.9 175.2 %reduce-scatter.6.cloned.1.call-start = ((), (), s32[]{:S(2)}) async-start(), calls=%async_computation.4 | async-start | bytes 393216 | tf_op jit(solution)/shard_map/reduce_scatter | solution.py:44
  192.9 149.8 %reduce-scatter.8.cloned.1.call-start = ((), (), s32[]{:S(2)}) async-start(), calls=%async_computation.5 | async-start | bytes 557056 | tf_op jit(solution)/shard_map/reduce_scatter | solution.py:77
Sparse Core Ops, SparseCore 0:
  22.0 10.4 reduce-scatter.3
  193.0 4.0 reduce-scatter.5
  265.4 77.2 reduce-scatter.7
where the time goes:
time: 351 us; the launch traced here: 350 us
  blocking collectives  169 us (48%)
  waiting for transfers between devices  90.3 us (26%)
  other arithmetic  53.9 us (15%)
  matrix products  14.9 us (4%)
  between operations  14.7 us (4%)
  local copies, waits for them, and re-layouts  7.35 us (2%)
    psum x1, blocking collectives, local(): next_basis = lax.psum(partial_value, 'cell').astype(jnp.bfloat16)  81.7 us
    psum x2, blocking collectives, first_total(): return lax.psum(gram, ('cell', 'gene'))  81.3 us
    reduce_scatter x1, waiting for transfers between devices, local(): lax.psum_scatter(loadings_of(final_rows), 'cell', scatter_dimension=1, ti...  75.5 us
    reduce_scatter x2, waiting for transfers between devices, merge_halves(): lax.psum_scatter(partial_scores, 'gene', scatter_dimension=1, tiled=True)  14.7 us
    scatter-add x2, other arithmetic, scores_of(): jax.ops.segment_sum(products, row_target, num_segments=row_blocks + 1)  14.1 us
    scatter-add x2, other arithmetic, loadings_of(): jax.ops.segment_sum(products, col_target, num_segments=gene_blocks + 1)  14.1 us
    another operation x6, other arithmetic, orthonormal(): lower_one = jnp.linalg.cholesky(first)  13 us
    another operation x4, other arithmetic, solve_lower(): return lax.linalg.triangular_solve(lower, right, left_side=True, lower=True)  11.1 us
  transfers between devices with their start and end apart: 3, of which 3 were waited for; matrix products, arithmetic and copies ran while one was open for 0% of the time, Pallas kernels for 0%

commit v1 on v0

--- a/solution.py
+++ b/solution.py
@@ -65,7 +65,7 @@
     ortho_half = ortho.astype(jnp.bfloat16)
     ortho_rows = lax.all_gather(ortho_half, "gene", axis=1, tiled=True)
     partial_value = loadings_of(ortho_rows)
-    next_basis = lax.psum(partial_value, "cell").astype(jnp.bfloat16)
+    next_basis = jnp.sum(lax.all_gather(partial_value, "cell"), axis=0).astype(jnp.bfloat16)
     ortho_two = orthonormal(scores_of(next_basis), first_total)
     scale = jnp.sqrt(jnp.float32(lax.axis_size("cell") * cell_dev))
     ortho_two_half = ortho_two.astype(jnp.bfloat16)

time: 351 us -> 389 us (1.11)
  waiting for transfers between devices: 90.3 us -> 204 us
  blocking collectives: 169 us -> 87 us
  other arithmetic: 53.9 us -> 57.8 us
    all_gather x0 -> x1, waiting for transfers between devices: none -> 112 us  [local(): lax.all_gather(partial_value, 'cell')]
    psum x1 -> x0, blocking collectives: 81.7 us -> none  [local(): next_basis = lax.psum(partial_value, 'cell').astype(jnp.bfloat16)]
    reduce_sum x0 -> x1, other arithmetic: none -> 3.96 us  [local(): jnp.sum(lax.all_gather(partial_value, 'cell'), axis=0).astype(jnp.bfloat16)]
  transfers between devices with their start and end apart: 3 -> 4, of which waited for: 3 -> 4; matrix products, arithmetic and copies ran while one was open for 0% -> 0% of each run, Pallas kernels for 0% -> 0%
where the time goes in v1:
time: 389 us; the launch traced here: 388 us
  waiting for transfers between devices  204 us (52%)
  blocking collectives  87 us (22%)
  other arithmetic  57.8 us (15%)
  matrix products  14.9 us (4%)
  between operations  14.7 us (4%)
  local copies, waits for them, and re-layouts  8.59 us (2%)
    all_gather x1, waiting for transfers between devices, local(): lax.all_gather(partial_value, 'cell')  112 us
    psum x2, blocking collectives, first_total(): return lax.psum(gram, ('cell', 'gene'))  81.3 us
    reduce_scatter x1, waiting for transfers between devices, local(): lax.psum_scatter(loadings_of(final_rows), 'cell', scatter_dimension=1, ti...  75.5 us
    reduce_scatter x2, waiting for transfers between devices, merge_halves(): lax.psum_scatter(partial_scores, 'gene', scatter_dimension=1, tiled=True)  16.5 us
    scatter-add x2, other arithmetic, scores_of(): jax.ops.segment_sum(products, row_target, num_segments=row_blocks + 1)  14.1 us
    scatter-add x2, other arithmetic, loadings_of(): jax.ops.segment_sum(products, col_target, num_segments=gene_blocks + 1)  14.1 us
    another operation x6, other arithmetic, orthonormal(): lower_one = jnp.linalg.cholesky(first)  13 us
    another operation x4, other arithmetic, solve_lower(): return lax.linalg.triangular_solve(lower, right, left_side=True, lower=True)  11.1 us
  transfers between devices with their start and end apart: 4, of which 4 were waited for; matrix products, arithmetic and copies ran while one was open for 0% of the time, Pallas kernels for 0%

profile of v1, /device:TPU:0, one launch (start us, length us, event | category | flops | bytes accessed | tf_op | source)
XLA Modules:
  0.0 387.7 jit_solution(13416190212108797483)
XLA Ops:
  7.2 0.8 compare_select_fusion
  8.0 0.7 compare_and_fusion
  8.7 1.0 copy_bitcast_fusion.4
  10.4 0.7 gather_fusion
  11.2 2.9 fusion.6
  14.1 7.1 %scatter_fusion = f32[9,64,128]{2,1,0:T(8,128)S(1)} fusion(f32[9,64,128]{2,1,0:T(8,128)S(1)} %broadcast.69.clone, s32[64]{0:T(128)S(1)} %get-tuple-element.8, f32[64,64,128]{2,1,0:T(8,128)} %fusion.6), kind=kCustom, calls=%fused_computation.4 | custom fusion | flops 524288 | bytes 6291712 | tf_op jit(solution)/shard_map/scatter-add | solution.py:51
  21.2 0.7 copy_bitcast_fusion.2
  21.9 0.0 all-gather.2.cloned.1.call-start
  22.0 10.5 %reduce-scatter.4.cloned.1.call-done = f32[64,512]{1,0:T(8,128)} async-done(((f32[64,1024]{1,0:T(8,128)}), f32[64,512]{1,0:T(8,128)}) %reduce-scatter.4.cloned.1.call-update) | async-done | bytes 131088 | tf_op jit(solution)/shard_map/reduce_scatter | solution.py:44
  32.5 1.2 fusion.40
  33.8 40.5 %psum.14 = f32[64,64]{0,1:T(8,128)S(1)} all-reduce(f32[64,64]{0,1:T(8,128)S(1)} %fusion.40), channel_id=1, replica_groups=mesh['cell'=16,'gene'=2] {'cell','gene'}, use_global_device_ids=true, to_apply=%region_2.4 | all-reduce | flops 4096 | bytes 32768 | tf_op jit(solution)/shard_map/psum | solution.py:41
  74.3 0.1 copy.32
  74.4 5.8 %cholesky.44 = f32[64,64]{1,0:T(8,128)S(1)} custom-call(f32[64,64]{1,0:T(8,128)S(1)} %fusion.30), custom_call_target="Cholesky" | custom-call | tf_op jit(solution)/shard_map/jit(cholesky)/cholesky | solution.py:21
  80.3 0.6 compare_reduce_fusion.1
  80.9 0.7 fusion.24
  81.6 4.9 %custom-call.6 = f32[1,64,64]{1,2,0:T(8,128)S(1)} custom-call(f32[1,64,64]{2,1,0:T(8,128)S(1)} %fusion.24), custom_call_target="InvertDiagBlocksLowerTriangular" | custom-call | tf_op jit(solution)/shard_map/triangular_solve/custom-call.0 | solution.py:10
  86.5 1.2 convolution_convert_fusion
  87.7 1.9 all_gather.12
  89.7 0.7 gather_fusion.1
  90.4 2.1 fusion.4
  92.6 7.1 %scatter_fusion.1 = f32[17,64,128]{2,1,0:T(8,128)S(1)} fusion(f32[17,64,128]{2,1,0:T(8,128)S(1)} %broadcast.70.clone, s32[64]{0:T(128)S(1)} %get-tuple-element.9, f32[64,64,128]{2,1,0:T(8,128)} %fusion.4), kind=kCustom, calls=%fused_computation.5 | custom fusion | flops 524288 | bytes 6291712 | tf_op jit(solution)/shard_map/scatter-add | solution.py:59
  99.7 0.3 copy.34
  100.0 0.9 all_gather_reshape.3
  101.0 112.3 %all-gather.2.cloned.1.call-done = f32[16,64,2048]{2,1,0:T(8,128)} async-done(((f32[1,64,2048]{2,1,0:T(8,128)}), f32[16,64,2048]{2,1,0:T(8,128)}) %all-gather.2.cloned.1.call-update) | async-done | bytes 8388624 | tf_op jit(solution)/shard_map/all_gather | solution.py:68
  213.3 4.0 %reduce_sum.9 = bf16[64,2048]{1,0:T(8,128)(2,1)S(1)} reduce(f32[16,64,2048]{2,1,0:T(8,128)} %all-gather.2.cloned.1.call-done, f32[]{:T(128)} %constant.55.clone.1), dimensions={0}, to_apply=%region_6.11 | reduce | flops 1966080 | bytes 8650756 | tf_op jit(solution)/shard_map/reduce_sum | solution.py:68
  217.3 0.1 copy_bitcast_fusion.3
  217.3 0.8 gather_fusion.2
  218.1 2.9 fusion.2
  221.0 7.1 %scatter_fusion.2 = f32[9,64,128]{2,1,0:T(8,128)S(1)} fusion(f32[9,64,128]{2,1,0:T(8,128)S(1)} %broadcast.69, s32[64]{0:T(128)S(1)} %get-tuple-element.8, f32[64,64,128]{2,1,0:T(8,128)} %fusion.2), kind=kCustom, calls=%fused_computation.6 | custom fusion | flops 524288 | bytes 6291712 | tf_op jit(solution)/shard_map/scatter-add | solution.py:51
  228.1 0.7 copy_bitcast_fusion.1
  228.8 0.0 reduce-scatter.8.cloned.1.call-start
  228.9 6.0 %reduce-scatter.6.cloned.1.call-done = f32[64,512]{1,0:T(8,128)} async-done(((f32[64,1024]{1,0:T(8,128)}), f32[64,512]{1,0:T(8,128)}) %reduce-scatter.6.cloned.1.call-update) | async-done | bytes 131088 | tf_op jit(solution)/shard_map/reduce_scatter | solution.py:44
  234.9 1.2 fusion.41
  236.1 40.8 %psum.15 = f32[64,64]{0,1:T(8,128)S(1)} all-reduce(f32[64,64]{0,1:T(8,128)S(1)} %fusion.41), channel_id=1, replica_groups=mesh['cell'=16,'gene'=2] {'cell','gene'}, use_global_device_ids=true, to_apply=%region_9.14 | all-reduce | flops 4096 | bytes 32768 | tf_op jit(solution)/shard_map/psum | solution.py:41
  276.9 0.1 copy.38
  277.0 5.8 %cholesky.55 = f32[64,64]{1,0:T(8,128)S(1)} custom-call(f32[64,64]{1,0:T(8,128)S(1)} %fusion.28), custom_call_target="Cholesky" | custom-call | tf_op jit(solution)/shard_map/jit(cholesky)/cholesky | solution.py:21
  282.9 0.6 compare_reduce_fusion
  283.5 0.7 fusion.25
  284.2 4.9 %custom-call.7 = f32[1,64,64]{1,2,0:T(8,128)S(1)} custom-call(f32[1,64,64]{2,1,0:T(8,128)S(1)} %fusion.25), custom_call_target="InvertDiagBlocksLowerTriangular" | custom-call | tf_op jit(solution)/shard_map/triangular_solve/custom-call.0 | solution.py:10
  289.1 1.2 fusion.39
  290.3 1.9 all_gather.15
  292.2 0.7 gather_fusion.3
  293.0 2.1 fusion
  295.1 7.1 %scatter_fusion.3 = f32[17,64,128]{2,1,0:T(8,128)S(1)} fusion(f32[17,64,128]{2,1,0:T(8,128)S(1)} %broadcast.70, s32[64]{0:T(128)S(1)} %get-tuple-element.9, f32[64,64,128]{2,1,0:T(8,128)} %fusion), kind=kCustom, calls=%fused_computation.7 | custom fusion | flops 524288 | bytes 6291712 | tf_op jit(solution)/shard_map/scatter-add | solution.py:59
  302.2 0.8 copy_bitcast_fusion
  303.1 1.9 all_gather.14
  305.0 75.5 %reduce-scatter.8.cloned.1.call-done = f32[64,128]{1,0:T(8,128)} async-done(((f32[64,2048]{1,0:T(8,128)}), f32[64,128]{1,0:T(8,128)}) %reduce-scatter.8.cloned.1.call-update) | async-done | bytes 32784 | tf_op jit(solution)/shard_map/reduce_scatter | solution.py:77
  380.5 0.7 copy.64
  (28 shorter events, 0.5 us)
Async XLA Ops:
  7.2 4.0 %copy-start = (bf16[1,64,128,128]{3,2,1,0:T(8,128)(2,1)S(1)}, bf16[1,64,128,128]{3,2,1,0:T(8,128)(2,1)}, u32[]{:S(2)}) copy-start(bf16[1,64,128,128]{3,2,1,0:T(8,128)(2,1)} %param.12) | copy-start | bytes 6291460
  7.2 4.0 %copy-start.1 = (s32[1,64]{1,0:T(1,128)S(1)}, s32[1,64]{1,0:T(1,128)}, u32[]{:S(2)}) copy-start(s32[1,64]{1,0:T(1,128)} %param.14) | copy-start | bytes 772
  7.2 4.0 %copy-start.2 = (s32[1,64]{1,0:T(1,128)S(1)}, s32[1,64]{1,0:T(1,128)}, u32[]{:S(2)}) copy-start(s32[1,64]{1,0:T(1,128)} %param.13) | copy-start | bytes 772
  7.2 25.3 %reduce-scatter.4.cloned.1.call-start = ((), (), s32[]{:S(2)}) async-start(), calls=%async_computation.3 | async-start | bytes 393216 | tf_op jit(solution)/shard_map/reduce_scatter | solution.py:44
  21.9 191.4 %all-gather.2.cloned.1.call-start = ((), (), s32[]{:S(2)}) async-start(), calls=%async_computation.4 | async-start | bytes 8912896 | tf_op jit(solution)/shard_map/all_gather | solution.py:68
  100.9 133.9 %reduce-scatter.6.cloned.1.call-start = ((), (), s32[]{:S(2)}) async-start(), calls=%async_computation.5 | async-start | bytes 393216 | tf_op jit(solution)/shard_map/reduce_scatter | solution.py:44
  228.8 151.7 %reduce-scatter.8.cloned.1.call-start = ((), (), s32[]{:S(2)}) async-start(), calls=%async_computation.6 | async-start | bytes 557056 | tf_op jit(solution)/shard_map/reduce_scatter | solution.py:77
Sparse Core Ops, SparseCore 0:
  22.0 10.4 reduce-scatter.3
  101.1 112.1 all-gather.1
  228.9 5.9 reduce-scatter.5
  303.2 77.2 reduce-scatter.7
